TPU v7x, 32 devices: a whole 2x2x4 slice. The times are simulated.
32 devices in a mesh: grp: 4 (over y, x), zero: 8 (over z, core).
Axes of the slice: x: 2, y: 2, z: 4, core: 2. Of those that a mesh axis runs over, the one named last changes fastest.
Arguments:
- replica_grads: bfloat16 [4, 3072, 2, 12288], P('grp', None, None, 'zero'), may hold values from -20000 to 20000, as said below
- master_weights: float32 [3072, 2, 12288], P(('grp', 'zero')), may hold values from -0.6 to 0.6
- first_moment: float32 [3072, 2, 12288], P(('grp', 'zero')), may hold values from -0.3 to 0.3
- second_moment: float32 [3072, 2, 12288], P(('grp', 'zero')), may hold values from 0.001 to 0.03
- max_norm: float32 [1], replicated, may hold values from 1737.7856 to 4344.464
Outputs:
- new_master: float32 [3072, 2, 12288], P(('grp', 'zero'))
- new_first: float32 [3072, 2, 12288], P(('grp', 'zero'))
- new_second: float32 [3072, 2, 12288], P(('grp', 'zero'))
- new_weights: bfloat16 [3072, 2, 12288], P(None, None, 'zero')
Inputs may be any that keep to these rules, and one draw needn't show every extreme that they name: `replica_grads`: one gradient of the joined weight for each replica group.
All inputs are finite; a program needn't handle non-finite values.
Results may differ from a plain program's by a relative error of at most 0.015.
Values may be sent and summed in bfloat16 or wider, within the bound.
A program may use at most 192 MiB of HBM per device.

v0:
```python
import jax
import jax.numpy as jnp
from jax import lax
from jax.sharding import PartitionSpec as P

ADAM_STEP = 10


beta_one = 0.9
beta_two = 0.95
learn_rate = 0.02
adam_eps = 1e-08
norm_eps = 1e-06


def adam_update(summed, master, first, second, scale):
    clipped = summed * scale
    new_first = beta_one * first + (1.0 - beta_one) * clipped
    new_second = beta_two * second + (1.0 - beta_two) * clipped * clipped
    correct_one = 1.0 - beta_one**ADAM_STEP
    correct_two = 1.0 - beta_two**ADAM_STEP
    step_size = new_first / correct_one / (jnp.sqrt(new_second / correct_two) + adam_eps)
    new_master = master - learn_rate * step_size
    return (new_master, new_first, new_second)


def body(replica_grads, master_weights, first_moment, second_moment, max_norm):
    groups = lax.axis_size("grp")
    shards = lax.axis_size("zero")
    local_grad = replica_grads[0]
    local_width = local_grad.shape[2]
    rows_dev = master_weights.shape[0]
    full_width = master_weights.shape[2]
    blocks = local_grad.reshape(groups, shards, rows_dev, 2, local_width)
    arrived = lax.all_to_all(
        lax.all_to_all(blocks[None], "grp", split_axis=1, concat_axis=0, tiled=True),
        "zero",
        split_axis=2,
        concat_axis=5,
        tiled=True,
    )
    summed = jnp.sum(arrived.astype(jnp.float32), axis=0)
    summed = summed.reshape(master_weights.shape)
    total = lax.psum(jnp.sum(summed * summed), ("grp", "zero"))
    scale = jnp.minimum(jnp.float32(1.0), max_norm[0] / (jnp.sqrt(total) + norm_eps))
    new_master, new_first, new_second = adam_update(
        summed, master_weights, first_moment, second_moment, scale
    )
    fresh = new_master.astype(jnp.bfloat16).reshape(1, 1, rows_dev, 2, full_width)
    own_tiles = lax.all_to_all(fresh, "zero", split_axis=4, concat_axis=1, tiled=True)
    tiled = lax.all_gather(own_tiles, "grp", axis=0, tiled=True)
    new_weights = tiled.reshape(groups * shards * rows_dev, 2, full_width // shards)
    return (new_master, new_first, new_second, new_weights)


def solution(mesh):
    in_specs = (
        P("grp", None, None, "zero"),
        P(("grp", "zero"), None, None),
        P(("grp", "zero"), None, None),
        P(("grp", "zero"), None, None),
        P(),
    )
    out_specs = (
        P(("grp", "zero"), None, None),
        P(("grp", "zero"), None, None),
        P(("grp", "zero"), None, None),
        P(None, None, "zero"),
    )
    return jax.shard_map(body, mesh=mesh, in_specs=in_specs, out_specs=out_specs, check_vma=False)
```

profile of v0, /device:TPU:0, one launch (start us, length us, event | category | flops | bytes accessed | tf_op | source)
XLA Modules:
  0.0 1264.3 jit_solution(17715620397299692491)
XLA Ops:
  7.2 0.0 all-gather.3.cloned.1.call-start
  7.2 218.8 %all_to_all.39 = bf16[1,4,8,96,2,1536]{5,4,3,2,0,1:T(2,128)(2,1)} all-to-all(bf16[1,4,8,96,2,1536]{5,4,3,2,0,1:T(2,128)(2,1)} %bitcast.20), channel_id=1, replica_groups=mesh['grp'=4,'zero'=8] {'grp'}, dimensions={1} | all-to-all | bytes 37748736 | tf_op jit(solution)/shard_map/all_to_all | solution.py:36
  226.0 15.4 %copy.48 = bf16[4,1,8,96,2,1536]{5,4,3,0,1,2:T(2,128)(2,1)S(1)} copy(bf16[4,1,8,96,2,1536]{5,4,3,2,0,1:T(2,128)(2,1)} %bitcast.16) | data formatting | bytes 37748736 | tf_op jit(solution)/shard_map/all_to_all | solution.py:36
  241.4 413.5 %all_to_all.40 = bf16[4,1,8,96,2,1536]{5,4,3,0,1,2:T(2,128)(2,1)} all-to-all(bf16[4,1,8,96,2,1536]{5,4,3,0,1,2:T(2,128)(2,1)S(1)} %copy.48), channel_id=1, replica_groups=mesh['grp'=4,'zero'=8] {'zero'}, dimensions={2} | all-to-all | bytes 37748736 | tf_op jit(solution)/shard_map/all_to_all | solution.py:35
  654.9 17.8 %convert_reduce_fusion = f32[8,96,2,1536]{3,1,2,0:T(8,128)} fusion(bf16[4,1,8,96,2,1536]{5,4,3,0,1,2:T(2,128)(2,1)} %all_to_all.40), kind=kLoop, calls=%fused_computation | loop fusion | flops 16515072 | bytes 28311552 | tf_op jit(solution)/shard_map/reduce_sum | solution.py:42
  672.7 14.0 %multiply_reduce_fusion = f32[]{:T(128)} fusion(f32[8,96,2,1536]{3,1,2,0:T(8,128)} %convert_reduce_fusion), kind=kLoop, calls=%fused_computation.8 | loop fusion | flops 4718591 | bytes 9437188 | tf_op jit(solution)/shard_map/reduce_sum | solution.py:44
  687.3 37.8 %psum.7 = f32[]{:T(128)} all-reduce(f32[]{:T(128)} %multiply_reduce_fusion), channel_id=1, replica_groups=mesh['grp'=4,'zero'=8] {'grp','zero'}, use_global_device_ids=true, to_apply=%region_2.0 | all-reduce | flops 1 | bytes 8 | tf_op jit(solution)/shard_map/psum | solution.py:44
  725.9 16.1 %multiply_bitcast_fusion = f32[96,2,8,1536]{3,1,0,2:T(2,128)S(1)} fusion(f32[8,96,2,1536]{3,1,2,0:T(8,128)} %convert_reduce_fusion, f32[]{:T(128)S(6)} %min_shard_map.3), kind=kLoop, calls=%fused_computation.7 | loop fusion | flops 2359296 | bytes 18874372 | tf_op jit(solution)/shard_map/mul | solution.py:17
  742.0 9.2 copy.51
  751.2 10.0 mul.56
  761.2 33.4 %convert_bitcast_fusion = (bf16[1,1,96,2,12288]{4,2,3,1,0:T(8,128)(2,1)}, f32[96,2,12288]{2,0,1:T(8,128)}, f32[96,2,12288]{2,0,1:T(8,128)}, f32[96,2,12288]{2,0,1:T(8,128)}) fusion(f32[96,2,12288]{2,1,0:T(2,128)} %param.6, f32[96,2,12288]{2,0,1:T(8,128)} %mul.56, f32[96,2,12288]{2,1,0:T(2,128)} %param.7, f32[96,2,12288]{2,1,0:T(2,128)} %param.8), kind=kLoop, calls=%fused_computation.9 | loop fusion | flops 33030144 | bytes 70778880 | tf_op jit(solution)/shard_map/reshape | solution.py:49
  794.7 14.1 %copy.54 = bf16[1,1,96,2,12288]{2,3,1,0,4:T(2,128)(2,1)} copy(bf16[1,1,96,2,12288]{4,2,3,1,0:T(8,128)(2,1)} %get-tuple-element.20) | data formatting | bytes 9437184 | tf_op jit(solution)/shard_map/reshape | solution.py:49
  808.7 144.7 %all_to_all.41 = bf16[1,1,96,2,12288]{2,3,1,0,4:T(2,128)(2,1)} all-to-all(bf16[1,1,96,2,12288]{2,3,1,0,4:T(2,128)(2,1)} %copy.54), channel_id=1, replica_groups=mesh['grp'=4,'zero'=8] {'zero'}, dimensions={4} | all-to-all | bytes 9437184 | tf_op jit(solution)/shard_map/all_to_all | solution.py:50
  953.5 15.8 %copy.55 = bf16[1,1,96,2,8,1536]{5,2,3,1,4,0:T(8,128)(2,1)} copy(bf16[1,1,96,2,8,1536]{2,3,5,4,1,0:T(2,128)(2,1)} %bitcast.19) | data formatting | bytes 9437184 | tf_op jit(solution)/shard_map/all_to_all | solution.py:50
  969.3 0.0 all-gather.3.cloned.1.call-update
  969.3 0.0 slice-start
  969.3 0.0 slice-start.1
  969.3 17.2 %copy.57 = f32[96,2,12288]{2,1,0:T(2,128)} copy(f32[96,2,12288]{2,0,1:T(8,128)} %get-tuple-element.21) | data formatting | bytes 18874368
  986.5 0.0 slice-start.2
  986.5 17.1 %copy.58 = f32[96,2,12288]{2,1,0:T(2,128)} copy(f32[96,2,12288]{2,0,1:T(8,128)} %get-tuple-element.22) | data formatting | bytes 18874368
  1003.7 0.0 slice-done
  1003.7 0.0 slice-done.1
  1003.7 0.0 slice-done.2
  1003.7 16.1 %copy.59 = f32[96,2,12288]{2,1,0:T(2,128)} copy(f32[96,2,12288]{2,0,1:T(8,128)S(1)} %bitcast.18) | data formatting | bytes 18874368
  1019.8 124.6 %all-gather.3.cloned.1.call-done = bf16[4,8,1,96,2,1536]{5,3,4,2,1,0:T(8,128)(2,1)} async-done(((bf16[1,8,1,96,2,1536]{5,3,4,2,1,0:T(8,128)(2,1)}), bf16[4,8,1,96,2,1536]{5,3,4,2,1,0:T(8,128)(2,1)}) %all-gather.3.cloned.1.call-update) | async-done | bytes 18874384 | tf_op jit(solution)/shard_map/all_gather | solution.py:51
  1144.3 9.5 copy.56
  1153.8 103.4 %copy.60 = bf16[3072,2,1536]{2,1,0:T(2,128)(2,1)} copy(bf16[3072,2,1536]{2,0,1:T(8,128)(2,1)S(1)} %bitcast.15) | data formatting | bytes 37748736
  (1 shorter events, 0.0 us)
Async XLA Ops:
  7.2 1137.2 %all-gather.3.cloned.1.call-start = ((), (), s32[]{:S(2)}) async-start(), calls=%async_computation.3 | async-start | bytes 23592960 | tf_op jit(solution)/shard_map/all_gather | solution.py:51
  969.3 34.4 %slice-start = ((s8[9437184]{0:T(1024)(128)(4,1)}), s8[4194304]{0:T(1024)(128)(4,1)S(1)}, s32[]{:S(2)}) async-start(s8[9437184]{0:T(1024)(128)(4,1)} %bitcast.17), calls=%async_computation.4 | async-start | bytes 8388608
  969.3 34.4 %slice-start.1 = ((s8[9437184]{0:T(1024)(128)(4,1)}), s8[4194304]{0:T(1024)(128)(4,1)S(1)}, s32[]{:S(2)}) async-start(s8[9437184]{0:T(1024)(128)(4,1)} %bitcast.17), calls=%async_computation.5 | async-start | bytes 8388608
  986.5 17.2 %slice-start.2 = ((s8[9437184]{0:T(1024)(128)(4,1)}), s8[1048576]{0:T(1024)(128)(4,1)S(1)}, s32[]{:S(2)}) async-start(s8[9437184]{0:T(1024)(128)(4,1)} %bitcast.17), calls=%async_computation.6 | async-start | bytes 2097152
Sparse Core Ops, SparseCore 0:
  969.4 174.8 all-gather.2
where the time goes:
time: 1270 us; the launch traced here: 1260 us
  blocking collectives  815 us (64%)
  local copies, waits for them, and re-layouts  228 us (18%)
  waiting for transfers between devices  125 us (10%)
  other arithmetic  81.3 us (6%)
  between operations  15.7 us (1%)
    all_to_all x1, blocking collectives, body(): lax.all_to_all(lax.all_to_all(blocks[None], 'grp', split_axis=1, concat_a...  414 us
    all_to_all x1, blocking collectives, body(): lax.all_to_all(blocks[None], 'grp', split_axis=1, concat_axis=0, tiled=True)  219 us
    unnamed x10, local copies, waits for them, and re-layouts  154 us
    all_to_all x1, blocking collectives, body(): lax.all_to_all(fresh, 'zero', split_axis=4, concat_axis=1, tiled=True)  145 us
    all_gather x1, waiting for transfers between devices, body(): tiled = lax.all_gather(own_tiles, 'grp', axis=0, tiled=True)  125 us
    psum x1, blocking collectives, body(): total = lax.psum(jnp.sum(summed * summed), ('grp', 'zero'))  37.8 us
    reshape x1, other arithmetic, body(): new_master.astype(jnp.bfloat16).reshape(1, 1, rows_dev, 2, full_width)  33.4 us
  transfers between devices with their start and end apart: 1, of which 1 were waited for; matrix products, arithmetic and copies ran while one was open for 4% of the time, Pallas kernels for 0%

commit v1 on v0

--- a/solution.py
+++ b/solution.py
@@ -1,10 +1,16 @@
+import functools
+
 import jax
 import jax.numpy as jnp
 from jax import lax
+from jax.experimental import pallas as pl
+from jax.experimental.pallas import tpu as pltpu
+from jax.experimental.layout import Layout, with_layout_constraint
 from jax.sharding import PartitionSpec as P
 
 ADAM_STEP = 10
-
+MESH = pl.DeviceIdType.MESH
+LANES = 128
 
 beta_one = 0.9
 beta_two = 0.95
@@ -24,7 +30,7 @@
     return (new_master, new_first, new_second)
 
 
-def body(replica_grads, master_weights, first_moment, second_moment, max_norm):
+def plain_body(replica_grads, master_weights, first_moment, second_moment, max_norm):
     groups = lax.axis_size("grp")
     shards = lax.axis_size("zero")
     local_grad = replica_grads[0]
@@ -53,6 +59,294 @@
     return (new_master, new_first, new_second, new_weights)
 
 
+def flip(index, mask, size):
+    out = 0
+    bit = 1
+    while bit < size:
+        b = (index // bit) % 2
+        out = out + bit * ((1 - b) if mask & bit else b)
+        bit *= 2
+    return out
+
+
+def greet(groups, shards, g, z):
+    barrier = pltpu.get_barrier_semaphore()
+    for k in range(1, shards):
+        pl.semaphore_signal(barrier, inc=1, device_id=(g, flip(z, k, shards)), device_id_type=MESH)
+    for j in range(1, groups):
+        pl.semaphore_signal(barrier, inc=1, device_id=(flip(g, j, groups), z), device_id_type=MESH)
+    pl.semaphore_wait(barrier, shards + groups - 2)
+
+
+def remote(src, dst, send, recv, device):
+    return pltpu.make_async_remote_copy(
+        src_ref=src, dst_ref=dst, send_sem=send, recv_sem=recv,
+        device_id=device, device_id_type=MESH,
+    )
+
+
+def scatter_kernel(groups, shards, grad, landed, norm, parts, own, sums, zone, gone,
+                   p_send, p_recv, own_sem, s_send, s_recv, nz_send, nz_recv, ng_send, ng_recv, loc_sem):
+    g, z = lax.axis_index("grp"), lax.axis_index("zero")
+    rows = own.shape[1]
+    order = list(range(shards - 1, -1, -1))
+
+    def part(j, k):
+        to = flip(g, j, groups)
+        return remote(grad.at[to, flip(z, k, shards)], parts.at[j - 1, k],
+                      p_send.at[j - 1, k], p_recv.at[j - 1, k], (to, z))
+
+    def mine(k):
+        return pltpu.make_async_copy(grad.at[g, flip(z, k, shards)], own.at[k], own_sem.at[k])
+
+    def onward(k):
+        return remote(sums.at[k], landed.at[z], s_send.at[k], s_recv.at[k], (g, flip(z, k, shards)))
+
+    for k in order:
+        mine(k).start()
+    greet(groups, shards, g, z)
+    for k in order:
+        for j in range(1, groups):
+            part(j, k).start()
+    stay = pltpu.make_async_copy(sums.at[0], landed.at[z], loc_sem)
+    square = jnp.zeros(own.shape[2:], jnp.float32)
+    for k in order:
+        mine(k).wait()
+        for j in range(1, groups):
+            part(j, k).wait_recv()
+
+        def add(r, acc, k=k):
+            total = own[k, r].astype(jnp.float32)
+            for j in range(1, groups):
+                total = total + parts[j - 1, k, r].astype(jnp.float32)
+            sums[k, r] = total.astype(jnp.bfloat16)
+            return acc + total * total
+
+        square = lax.fori_loop(0, rows, add, square)
+        if k:
+            onward(k).start()
+        else:
+            stay.start()
+
+    folded = square[0:8]
+    for i in range(8, square.shape[0], 8):
+        folded = folded + square[i:i + 8]
+    zone[0] = folded
+
+    def tell_zero(k):
+        return remote(zone.at[0], zone.at[k], nz_send.at[k], nz_recv.at[k], (g, flip(z, k, shards)))
+
+    def tell_group(j):
+        return remote(gone.at[0], gone.at[j], ng_send.at[j], ng_recv.at[j], (flip(g, j, groups), z))
+
+    for k in range(1, shards):
+        tell_zero(k).start()
+    for k in range(1, shards):
+        tell_zero(k).wait_recv()
+    gone[0] = jnp.sum(zone[...], axis=0)
+    for j in range(1, groups):
+        tell_group(j).start()
+    for j in range(1, groups):
+        tell_group(j).wait_recv()
+    norm[...] = jnp.sum(gone[...], axis=0)
+
+    for k in range(1, shards):
+        tell_zero(k).wait_send()
+    for j in range(1, groups):
+        tell_group(j).wait_send()
+    for k in order:
+        for j in range(1, groups):
+            part(j, k).wait_send()
+        if k:
+            onward(k).wait()
+        else:
+            stay.wait()
+
+
+def update_kernel(limit, norm, summed, master, first, second, out_master, out_first, out_second, fresh):
+    total = jnp.full(master.shape[2:], jnp.sum(norm[...]), jnp.float32)
+    scale = jnp.minimum(jnp.float32(1.0), limit[0] / (jnp.sqrt(total) + norm_eps))
+
+    def row(r, carry):
+        for c in range(summed.shape[0]):
+            new_master, new_first, new_second = adam_update(
+                summed[c, r].astype(jnp.float32), master[r, c], first[r, c], second[r, c], scale
+            )
+            out_master[r, c] = new_master
+            out_first[r, c] = new_first
+            out_second[r, c] = new_second
+            fresh[c, r] = new_master.astype(jnp.bfloat16)
+        return carry
+
+    lax.fori_loop(0, master.shape[0], row, 0)
+
+
+def gather_kernel(groups, shards, fresh, out, hold, z_send, z_recv, x_send, x_recv, y_send, y_recv,
+                  u_send, u_recv, v_send, v_recv, loc_sem):
+    g, z = lax.axis_index("grp"), lax.axis_index("zero")
+    half = fresh.shape[1] // 2
+    gx, gy = flip(g, 1, groups), flip(g, 2, groups)
+
+    def spread(k):
+        return remote(fresh.at[flip(z, k, shards)], out.at[g, z], z_send.at[k], z_recv.at[k],
+                      (g, flip(z, k, shards)))
+
+    def first_hop(k, send, recv, to):
+        q = flip(z, k, shards)
+        src = out.at[g, q] if k else fresh.at[z]
+        return remote(src, out.at[g, q], send.at[k], recv.at[k], (to, z))
+
+    def second_hop(k, origin, start, send, recv, to):
+        q = flip(z, k, shards)
+        ref = out.at[origin, q, pl.ds(start, half)]
+        return remote(ref, ref, send.at[k], recv.at[k], (to, z))
+
+    def hops(k):
+        return (first_hop(k, x_send, x_recv, gx), first_hop(k, y_send, y_recv, gy))
+
+    def turns(k):
+        return (second_hop(k, gx, 0, u_send, u_recv, gy), second_hop(k, gy, half, v_send, v_recv, gx))
+
+    load = pltpu.make_async_copy(fresh.at[z], hold, loc_sem.at[0])
+    store = pltpu.make_async_copy(hold, out.at[g, z], loc_sem.at[1])
+    load.start()
+    greet(groups, shards, g, z)
+    for k in range(1, shards):
+        spread(k).start()
+    lag = 1
+    for s in range(shards + lag):
+        if s < shards:
+            if s:
+                spread(s).wait_recv()
+            for hop in hops(s):
+                hop.start()
+            if s == 0:
+                load.wait()
+                store.start()
+        if s >= lag:
+            for hop, turn in zip(hops(s - lag), turns(s - lag)):
+                hop.wait_recv()
+                turn.start()
+    store.wait()
+    for k in range(shards):
+        if k:
+            spread(k).wait_send()
+        for hop in hops(k):
+            hop.wait_send()
+        for turn in turns(k):
+            turn.wait()
+
+
+def flat_body(replica_grads, master_weights, first_moment, second_moment, max_norm):
+    groups = lax.axis_size("grp")
+    shards = lax.axis_size("zero")
+    rows = master_weights.shape[0]
+    width = replica_grads.shape[3]
+    tiles = width // LANES
+    deep = 2 * tiles
+    bf16, f32 = jnp.bfloat16, jnp.float32
+    any_space = pl.BlockSpec(memory_space=pl.ANY)
+    dma = pltpu.SemaphoreType.DMA
+    limit = 60 * 1024 * 1024
+
+    def keep(x, *order):
+        return with_layout_constraint(x, Layout(major_to_minor=order))
+
+    def flat(x):
+        x = x.reshape(x.shape[0], 2, -1, LANES)
+        return jnp.swapaxes(keep(x, 0, 2, 1, 3), 1, 2)
+
+    grad = flat(replica_grads[0]).reshape(groups, shards, rows, deep, LANES)
+    master, first, second = (
+        flat(x).reshape(rows, shards, deep, LANES)
+        for x in (master_weights, first_moment, second_moment)
+    )
+
+    piece = (rows, deep, LANES)
+    landed, norm = pl.pallas_call(
+        functools.partial(scatter_kernel, groups, shards),
+        out_shape=(
+            jax.ShapeDtypeStruct((shards,) + piece, bf16),
+            jax.ShapeDtypeStruct((8, LANES), f32),
+        ),
+        in_specs=[any_space],
+        out_specs=(any_space, pl.BlockSpec(memory_space=pltpu.VMEM)),
+        scratch_shapes=[
+            pltpu.VMEM((groups - 1, shards) + piece, bf16),
+            pltpu.VMEM((shards,) + piece, bf16),
+            pltpu.VMEM((shards,) + piece, bf16),
+            pltpu.VMEM((shards, 8, LANES), f32),
+            pltpu.VMEM((groups, 8, LANES), f32),
+            dma((groups - 1, shards)),
+            dma((groups - 1, shards)),
+            dma((shards,)),
+            dma((shards,)),
+            dma((shards,)),
+            dma((shards,)),
+            dma((shards,)),
+            dma((groups,)),
+            dma((groups,)),
+            dma,
+        ],
+        compiler_params=pltpu.CompilerParams(
+            collective_id=0, has_side_effects=True, vmem_limit_bytes=limit
+        ),
+    )(grad)
+
+    step = 8 if rows % 8 == 0 else 1
+    by_row = pl.BlockSpec((step, shards, deep, LANES), lambda i: (i, 0, 0, 0))
+    by_shard = pl.BlockSpec((shards, step, deep, LANES), lambda i: (0, i, 0, 0))
+    state = jax.ShapeDtypeStruct((rows, shards, deep, LANES), f32)
+    new_master, new_first, new_second, fresh = pl.pallas_call(
+        update_kernel,
+        grid=(rows // step,),
+        out_shape=(state, state, state, jax.ShapeDtypeStruct((shards,) + piece, bf16)),
+        in_specs=[
+            pl.BlockSpec(memory_space=pltpu.SMEM),
+            pl.BlockSpec((8, LANES), lambda i: (0, 0)),
+            by_shard, by_row, by_row, by_row,
+        ],
+        out_specs=(by_row, by_row, by_row, by_shard),
+        compiler_params=pltpu.CompilerParams(vmem_limit_bytes=limit),
+    )(max_norm, norm, landed, master, first, second)
+
+    gathered = pl.pallas_call(
+        functools.partial(gather_kernel, groups, shards),
+        out_shape=jax.ShapeDtypeStruct((groups, shards) + piece, bf16),
+        in_specs=[any_space],
+        out_specs=any_space,
+        scratch_shapes=[pltpu.VMEM(piece, bf16)] + [dma((shards,))] * 10 + [dma((2,))],
+        compiler_params=pltpu.CompilerParams(
+            collective_id=1, has_side_effects=True, vmem_limit_bytes=limit
+        ),
+    )(fresh)
+
+    def unflat(x, shape):
+        x = x.reshape(shape[0], -1, 2, LANES)
+        return keep(jnp.swapaxes(x, 1, 2), 0, 2, 1, 3).reshape(shape)
+
+    shape = master_weights.shape
+    return (
+        unflat(new_master, shape),
+        unflat(new_first, shape),
+        unflat(new_second, shape),
+        unflat(gathered, replica_grads.shape[1:]),
+    )
+
+
+def body(replica_grads, master_weights, first_moment, second_moment, max_norm):
+    groups = lax.axis_size("grp")
+    shards = lax.axis_size("zero")
+    rows = master_weights.shape[0]
+    width = replica_grads.shape[3]
+    deep = 2 * width // LANES
+    power = shards > 1 and shards & (shards - 1) == 0
+    fits = groups * shards * rows * deep * LANES * 2 * 3 // 2 < 48 * 1024 * 1024
+    whole = width % LANES == 0 and deep % 8 == 0 and rows % 2 == 0
+    run = flat_body if groups == 4 and power and fits and whole else plain_body
+    return run(replica_grads, master_weights, first_moment, second_moment, max_norm)
+
+
 def solution(mesh):
     in_specs = (
         P("grp", None, None, "zero"),

time: 1270 us -> 430 us (0.34)
  blocking collectives: 815 us -> 0 us
  Pallas kernels: 0 us -> 413 us
  local copies, waits for them, and re-layouts: 228 us -> 15.8 us
  waiting for transfers between devices: 125 us -> 0 us
  other arithmetic: 81.3 us -> 0 us
  between operations: 15.7 us -> 1.29 us
    all_to_all x3 -> x0, blocking collectives: 777 us -> none  [the longest x1 414 us: body(): lax.all_to_all(lax.all_to_all(blocks[None], 'grp', split_axis=1, concat_a...]
    pallas_call x0 -> x3, Pallas kernels: none -> 413 us  [the longest x1 220 us: flat_body(): pl.pallas_call(functools.partial(scatter_kernel, groups, shards), out_sha...]
    unnamed x10 -> x1, local copies, waits for them, and re-layouts: 154 us -> 15.8 us
    all_gather x1 -> x0, waiting for transfers between devices: 125 us -> none  [body(): tiled = lax.all_gather(own_tiles, 'grp', axis=0, tiled=True)]
    psum x1 -> x0, blocking collectives: 37.8 us -> none  [body(): total = lax.psum(jnp.sum(summed * summed), ('grp', 'zero'))]
    reshape x1 -> x0, other arithmetic: 33.4 us -> none  [body(): new_master.astype(jnp.bfloat16).reshape(1, 1, rows_dev, 2, full_width)]
    reduce_sum x2 -> x0, other arithmetic: 31.8 us -> none  [the longest x1 17.8 us: body(): summed = jnp.sum(arrived.astype(jnp.float32), axis=0)]
    all_to_all x2 -> x0, local copies, waits for them, and re-layouts: 31.2 us -> none  [the longest x1 15.8 us: body(): lax.all_to_all(fresh, 'zero', split_axis=4, concat_axis=1, tiled=True)]
  transfers between devices with their start and end apart: 1 -> 0, of which waited for: 1 -> 0; matrix products, arithmetic and copies ran while one was open for 4% -> 0% of each run, Pallas kernels for 0% -> 0%
where the time goes in v1:
time: 430 us
  Pallas kernels  413 us (96%)
  local copies, waits for them, and re-layouts  15.8 us (4%)
    pallas_call x1, Pallas kernels, flat_body(): pl.pallas_call(functools.partial(scatter_kernel, groups, shards), out_sha...  220 us
    pallas_call x1, Pallas kernels, flat_body(): pl.pallas_call(functools.partial(gather_kernel, groups, shards), out_shap...  165 us
    pallas_call x1, Pallas kernels, flat_body(): pl.pallas_call(update_kernel, grid=(rows // step,), out_shape=(state, sta...  27.8 us
    unnamed x1, local copies, waits for them, and re-layouts  15.8 us

profile of v1, /device:TPU:0, one launch (start us, length us, event | category | flops | bytes accessed | tf_op | source)
XLA Modules:
  0.0 429.8 jit_solution(5495250775022953610)
XLA Ops:
  1.3 219.6 %shard_map.84 = (bf16[8,96,24,128]{3,2,1,0:T(8,128)(2,1)}, f32[8,128]{1,0:T(8,128)}) custom-call(bf16[4,8,96,24,128]{4,3,2,1,0:T(8,128)(2,1)} %bitcast.41), custom_call_target="tpu_custom_call" | custom-call | tf_op jit(solution)/shard_map/pallas_call | solution.py:266
  220.9 27.8 %shard_map.85 = (f32[96,8,24,128]{3,2,1,0:T(8,128)}, f32[96,8,24,128]{3,2,1,0:T(8,128)}, f32[96,8,24,128]{3,2,1,0:T(8,128)}, bf16[8,96,24,128]{3,2,1,0:T(8,128)(2,1)}) custom-call(f32[1]{0:T(128)S(6)} %copy.10.limit, f32[8,128]{1,0:T(8,128)} %get-tuple-element.10.norm, bf16[8,96,24,128]{3,2,1,0:T(8,128)(2,1)} %get-tuple-element.11.summed, ...), custom_call_target="tpu_custom_call" | custom-call | tf_op jit(solution)/shard_map/pallas_call | solution.py:300
  248.8 165.2 %shard_map.86 = bf16[4,8,96,24,128]{4,3,2,1,0:T(8,128)(2,1)} custom-call(bf16[8,96,24,128]{3,2,1,0:T(8,128)(2,1)} %get-tuple-element.15.fresh), custom_call_target="tpu_custom_call" | custom-call | tf_op jit(solution)/shard_map/pallas_call | solution.py:313
  414.0 15.8 %copy.11 = bf16[3072,2,1536]{2,1,0:T(2,128)(2,1)} copy(bf16[3072,2,1536]{2,1,0:T(2,128)(2,1)} %bitcast.40) | data formatting | bytes 37748736

commit v2 on v1

--- a/solution.py
+++ b/solution.py
@@ -85,48 +85,80 @@
     )
 
 
-def scatter_kernel(groups, shards, grad, landed, norm, parts, own, sums, zone, gone,
-                   p_send, p_recv, own_sem, s_send, s_recv, nz_send, nz_recv, ng_send, ng_recv, loc_sem):
+def scatter_kernel(groups, shards, grad, landed, norm, near, far, own, kept, pairs, got, sums, zone, gone,
+                   f_send, f_recv, load_sem, p_send, p_recv, s_send, s_recv,
+                   nz_send, nz_recv, ng_send, ng_recv, loc_sem):
     g, z = lax.axis_index("grp"), lax.axis_index("zero")
-    rows = own.shape[1]
+    gx, gy, diagonal = flip(g, 1, groups), flip(g, 2, groups), flip(g, 3, groups)
+    first_to, second_to = (gx, gy), (gy, gx)
+    rows = own.shape[2]
     order = list(range(shards - 1, -1, -1))
 
-    def part(j, k):
-        to = flip(g, j, groups)
-        return remote(grad.at[to, flip(z, k, shards)], parts.at[j - 1, k],
-                      p_send.at[j - 1, k], p_recv.at[j - 1, k], (to, z))
-
-    def mine(k):
-        return pltpu.make_async_copy(grad.at[g, flip(z, k, shards)], own.at[k], own_sem.at[k])
+    def raw(k, h, d):
+        block = diagonal if d else first_to[h]
+        return remote(grad.at[block, flip(z, k, shards), h], (far if d else near).at[k, h],
+                      f_send.at[k, h, d], f_recv.at[k, h, d], (first_to[h], z))
+
+    def pair(k, h):
+        return remote(pairs.at[k, h], got.at[k, h], p_send.at[k, h], p_recv.at[k, h], (second_to[h], z))
+
+    def load(k, h, d):
+        block = second_to[h] if d else g
+        return pltpu.make_async_copy(grad.at[block, flip(z, k, shards), h], (kept if d else own).at[k, h],
+                                     load_sem.at[k, h, d])
 
     def onward(k):
         return remote(sums.at[k], landed.at[z], s_send.at[k], s_recv.at[k], (g, flip(z, k, shards)))
 
+    def begin(k):
+        for d in (1, 0):
+            for h in (0, 1):
+                raw(k, h, d).start()
+
     for k in order:
-        mine(k).start()
+        for d in (1, 0):
+            for h in (0, 1):
+                load(k, h, d).start()
     greet(groups, shards, g, z)
-    for k in order:
-        for j in range(1, groups):
-            part(j, k).start()
+    ahead = 3
+    for k in order[:ahead]:
+        begin(k)
     stay = pltpu.make_async_copy(sums.at[0], landed.at[z], loc_sem)
-    square = jnp.zeros(own.shape[2:], jnp.float32)
-    for k in order:
-        mine(k).wait()
-        for j in range(1, groups):
-            part(j, k).wait_recv()
-
-        def add(r, acc, k=k):
-            total = own[k, r].astype(jnp.float32)
-            for j in range(1, groups):
-                total = total + parts[j - 1, k, r].astype(jnp.float32)
-            sums[k, r] = total.astype(jnp.bfloat16)
-            return acc + total * total
-
-        square = lax.fori_loop(0, rows, add, square)
-        if k:
-            onward(k).start()
-        else:
-            stay.start()
+    square = jnp.zeros(own.shape[3:], jnp.float32)
+    for i in range(shards + 1):
+        if i < shards:
+            k = order[i]
+            for h in (0, 1):
+                load(k, h, 1).wait()
+                raw(k, h, 1).wait_recv()
+
+                def join(r, carry, k=k, h=h):
+                    both = kept[k, h, r].astype(jnp.float32) + far[k, h, r].astype(jnp.float32)
+                    pairs[k, h, r] = both.astype(jnp.bfloat16)
+                    return carry
+
+                lax.fori_loop(0, rows, join, 0)
+                pair(k, h).start()
+            if i + ahead < shards:
+                begin(order[i + ahead])
+        if i >= 1:
+            k = order[i - 1]
+            for h in (0, 1):
+                load(k, h, 0).wait()
+                raw(k, h, 0).wait_recv()
+                pair(k, h).wait_recv()
+
+                def add(r, acc, k=k, h=h):
+                    total = own[k, h, r].astype(jnp.float32) + near[k, h, r].astype(jnp.float32)
+                    total = total + got[k, h, r].astype(jnp.float32)
+                    sums[k, h, r] = total.astype(jnp.bfloat16)
+                    return acc + total * total
+
+                square = lax.fori_loop(0, rows, add, square)
+            if k:
+                onward(k).start()
+            else:
+                stay.start()
 
     folded = square[0:8]
     for i in range(8, square.shape[0], 8):
@@ -155,8 +187,10 @@
     for j in range(1, groups):
         tell_group(j).wait_send()
     for k in order:
-        for j in range(1, groups):
-            part(j, k).wait_send()
+        for h in (0, 1):
+            pair(k, h).wait_send()
+            for d in (0, 1):
+                raw(k, h, d).wait_send()
         if k:
             onward(k).wait()
         else:
@@ -167,11 +201,16 @@
     total = jnp.full(master.shape[2:], jnp.sum(norm[...]), jnp.float32)
     scale = jnp.minimum(jnp.float32(1.0), limit[0] / (jnp.sqrt(total) + norm_eps))
 
+    rate_one = learn_rate / (1.0 - beta_one**ADAM_STEP)
+    over_two = 1.0 / (1.0 - beta_two**ADAM_STEP)
+
     def row(r, carry):
         for c in range(summed.shape[0]):
-            new_master, new_first, new_second = adam_update(
-                summed[c, r].astype(jnp.float32), master[r, c], first[r, c], second[r, c], scale
-            )
+            clipped = summed[c, r].astype(jnp.float32) * scale
+            new_first = beta_one * first[r, c] + (1.0 - beta_one) * clipped
+            new_second = beta_two * second[r, c] + (1.0 - beta_two) * clipped * clipped
+            below = jnp.sqrt(new_second * over_two) + adam_eps
+            new_master = master[r, c] - new_first * rate_one / below
             out_master[r, c] = new_master
             out_first[r, c] = new_first
             out_second[r, c] = new_second
@@ -256,34 +295,29 @@
         x = x.reshape(x.shape[0], 2, -1, LANES)
         return jnp.swapaxes(keep(x, 0, 2, 1, 3), 1, 2)
 
-    grad = flat(replica_grads[0]).reshape(groups, shards, rows, deep, LANES)
+    grad = flat(replica_grads[0]).reshape(groups, shards, 2, rows // 2, deep, LANES)
     master, first, second = (
         flat(x).reshape(rows, shards, deep, LANES)
         for x in (master_weights, first_moment, second_moment)
     )
 
     piece = (rows, deep, LANES)
+    halves = (shards, 2, rows // 2, deep, LANES)
     landed, norm = pl.pallas_call(
         functools.partial(scatter_kernel, groups, shards),
         out_shape=(
-            jax.ShapeDtypeStruct((shards,) + piece, bf16),
+            jax.ShapeDtypeStruct(halves, bf16),
             jax.ShapeDtypeStruct((8, LANES), f32),
         ),
         in_specs=[any_space],
         out_specs=(any_space, pl.BlockSpec(memory_space=pltpu.VMEM)),
         scratch_shapes=[
-            pltpu.VMEM((groups - 1, shards) + piece, bf16),
-            pltpu.VMEM((shards,) + piece, bf16),
-            pltpu.VMEM((shards,) + piece, bf16),
+            *[pltpu.VMEM(halves, bf16)] * 7,
             pltpu.VMEM((shards, 8, LANES), f32),
             pltpu.VMEM((groups, 8, LANES), f32),
-            dma((groups - 1, shards)),
-            dma((groups - 1, shards)),
-            dma((shards,)),
-            dma((shards,)),
-            dma((shards,)),
-            dma((shards,)),
-            dma((shards,)),
+            *[dma((shards, 2, 2))] * 3,
+            *[dma((shards, 2))] * 2,
+            *[dma((shards,))] * 4,
             dma((groups,)),
             dma((groups,)),
             dma,
@@ -308,7 +342,7 @@
         ],
         out_specs=(by_row, by_row, by_row, by_shard),
         compiler_params=pltpu.CompilerParams(vmem_limit_bytes=limit),
-    )(max_norm, norm, landed, master, first, second)
+    )(max_norm, norm, landed.reshape((shards,) + piece), master, first, second)
 
     gathered = pl.pallas_call(
         functools.partial(gather_kernel, groups, shards),
@@ -341,7 +375,7 @@
     width = replica_grads.shape[3]
     deep = 2 * width // LANES
     power = shards > 1 and shards & (shards - 1) == 0
-    fits = groups * shards * rows * deep * LANES * 2 * 3 // 2 < 48 * 1024 * 1024
+    fits = groups * shards * rows * deep * LANES * 2 * 7 // 4 < 48 * 1024 * 1024
     whole = width % LANES == 0 and deep % 8 == 0 and rows % 2 == 0
     run = flat_body if groups == 4 and power and fits and whole else plain_body
     return run(replica_grads, master_weights, first_moment, second_moment, max_norm)

time: 430 us -> 396 us (0.921)
  Pallas kernels: 413 us -> 378 us
    pallas_call x1, Pallas kernels: 220 us -> 186 us  [flat_body(): pl.pallas_call(functools.partial(scatter_kernel, groups, shards), out_sha...]
where the time goes in v2:
time: 396 us; the launch traced here: 395 us
  Pallas kernels  378 us (95%)
  local copies, waits for them, and re-layouts  15.8 us (4%)
    pallas_call x1, Pallas kernels, flat_body(): pl.pallas_call(functools.partial(scatter_kernel, groups, shards), out_sha...  186 us
    pallas_call x1, Pallas kernels, flat_body(): pl.pallas_call(functools.partial(gather_kernel, groups, shards), out_shap...  164 us
    pallas_call x1, Pallas kernels, flat_body(): pl.pallas_call(update_kernel, grid=(rows // step,), out_shape=(state, sta...  27.7 us
    unnamed x1, local copies, waits for them, and re-layouts  15.8 us

profile of v2, /device:TPU:0, one launch (start us, length us, event | category | flops | bytes accessed | tf_op | source)
XLA Modules:
  0.0 395.3 jit_solution(2341277688619584491)
XLA Ops:
  1.3 186.1 %shard_map.84 = (bf16[8,2,48,24,128]{4,3,2,1,0:T(8,128)(2,1)}, f32[8,128]{1,0:T(8,128)}) custom-call(bf16[4,8,2,48,24,128]{5,4,3,2,1,0:T(8,128)(2,1)} %bitcast.42), custom_call_target="tpu_custom_call" | custom-call | tf_op jit(solution)/shard_map/pallas_call | solution.py:306
  187.3 27.7 %shard_map.85 = (f32[96,8,24,128]{3,2,1,0:T(8,128)}, f32[96,8,24,128]{3,2,1,0:T(8,128)}, f32[96,8,24,128]{3,2,1,0:T(8,128)}, bf16[8,96,24,128]{3,2,1,0:T(8,128)(2,1)}) custom-call(f32[1]{0:T(128)S(6)} %copy.10.limit, f32[8,128]{1,0:T(8,128)} %get-tuple-element.10.norm, bf16[8,96,24,128]{3,2,1,0:T(8,128)(2,1)} %bitcast.46, f32[96,8,24,128]{3,2,1,0:T(8,128)} %bitcast.43, ...), custom_call_target="tpu_custom_call" | custom-call | tf_op jit(solution)/shard_map/pallas_call | solution.py:334
  215.0 164.4 %shard_map.86 = bf16[4,8,96,24,128]{4,3,2,1,0:T(8,128)(2,1)} custom-call(bf16[8,96,24,128]{3,2,1,0:T(8,128)(2,1)} %get-tuple-element.15.fresh), custom_call_target="tpu_custom_call" | custom-call | tf_op jit(solution)/shard_map/pallas_call | solution.py:347
  379.5 15.8 %copy.11 = bf16[3072,2,1536]{2,1,0:T(2,128)(2,1)} copy(bf16[3072,2,1536]{2,1,0:T(2,128)(2,1)} %bitcast.41) | data formatting | bytes 37748736
